TPU v7x, 32 devices: a whole 2x2x4 slice. The times are simulated.
32 devices in a mesh: ctx: 8 (over z, x), tp: 4 (over y, core).
Axes of the slice: x: 2, y: 2, z: 4, core: 2. Of those that a mesh axis runs over, the one named last changes fastest.
Arguments:
- hidden_in: bfloat16 [4096, 5376], P(('ctx', 'tp')), may hold values from -6 to 6
- stretch_start: int32 [1], replicated, may hold values from 1 to 1024
- pre_gain: float32 [5376], replicated, may hold values from 0.1 to 1.9
- q_weight: bfloat16 [5376, 4096], P('ctx', 'tp'), may hold values from -1 to 1
- k_weight: bfloat16 [5376, 2048], P('ctx', 'tp'), may hold values from -1 to 1
- v_weight: bfloat16 [5376, 2048], P('ctx', 'tp'), may hold values from -0.078125 to 0.078125
- o_weight: bfloat16 [4096, 5376], P('tp', 'ctx'), may hold values from -0.09375 to 0.09375
- q_gain: float32 [128], replicated, may hold values from 0.5 to 5
- k_gain: float32 [128], replicated, may hold values from 0.5 to 5
- prior_keys: bfloat16 [1024, 2048], P(None, 'tp'), may hold values from -6 to 6
- prior_values: bfloat16 [1024, 2048], P(None, 'tp'), may hold values from -6 to 6
- post_gain: float32 [5376], replicated, may hold values from 0.1 to 1.9
Outputs:
- result: bfloat16 [4096, 5376], P(('ctx', 'tp'))
All inputs are finite; a program needn't handle non-finite values.
Results may differ from a plain program's by a relative error of at most 0.013.
Values may be sent and summed in bfloat16 or wider, within the bound.
No kernel may reach another device: no remote copies, remote signals or barrier semaphores. Data moves between devices by JAX's collectives and lax.ppermute only.
A program may use at most 128 MiB of HBM per device.

v0:
```python
import jax
import jax.numpy as jnp
from jax import lax
from jax.sharding import PartitionSpec as P

HD = 128
WINDOW = 1024
EPSILON = 1e-06
QUERY_FACTOR = 168.0 ** (-0.5)


def from_behind(value, axis, steps):
    count = lax.axis_size(axis)
    leading, last = (max(0, -steps), min(count, count - steps))
    return lax.ppermute(value, axis, [(source, source + steps) for source in range(leading, last)])


def rms_scale(inputs, scales):
    mean_sq = jnp.mean(inputs * inputs, axis=-1, keepdims=True)
    return inputs * lax.rsqrt(mean_sq + EPSILON) * scales


def rotate(inputs, positions):
    half_dim = inputs.shape[-1] // 2
    frequency = 10000.0 ** (-jnp.arange(half_dim, dtype=jnp.float32) / half_dim)
    angles = positions.astype(jnp.float32)[:, None] * frequency[None, :]
    cosines = jnp.cos(angles)[:, None, :]
    sines = jnp.sin(angles)[:, None, :]
    front = inputs[..., :half_dim]
    second = inputs[..., half_dim:]
    return jnp.concatenate(
        [front * cosines - second * sines, second * cosines + front * sines], axis=-1
    )


def local(
    hidden_in,
    stretch_start,
    pre_gain,
    q_weight,
    k_weight,
    v_weight,
    o_weight,
    q_gain,
    k_gain,
    prior_keys,
    prior_values,
    post_gain,
):
    residual_in = hidden_in.astype(jnp.float32)
    normed = rms_scale(residual_in, pre_gain).astype(jnp.bfloat16)
    block_rows = lax.all_gather(normed, "tp", axis=0, tiled=True)
    row_count = block_rows.shape[0]
    query_cols = q_weight.shape[1]
    kv_cols = k_weight.shape[1]

    def add_piece(segment):
        return jnp.dot(block_rows, segment, preferred_element_type=jnp.float32)

    query_raw = add_piece(lax.all_gather(q_weight, "ctx", axis=0, tiled=True))
    key_raw = add_piece(lax.all_gather(k_weight, "ctx", axis=0, tiled=True))
    value_raw = add_piece(lax.all_gather(v_weight, "ctx", axis=0, tiled=True))
    local_heads = query_cols // HD
    local_kv = kv_cols // HD
    group = local_heads // local_kv
    chain_pos = lax.axis_index("ctx")
    positions = WINDOW + chain_pos * row_count + jnp.arange(row_count, dtype=jnp.int32)
    query = (
        rotate(rms_scale(query_raw.reshape(row_count, local_heads, HD), q_gain), positions)
        * QUERY_FACTOR
    ).astype(jnp.bfloat16)
    key_rows = (
        rotate(rms_scale(key_raw.reshape(row_count, local_kv, HD), k_gain), positions)
        .astype(jnp.bfloat16)
        .reshape(row_count, kv_cols)
    )
    value_rows = value_raw.astype(jnp.bfloat16)
    reach = WINDOW // row_count
    earlier = [
        from_behind((key_rows, value_rows), "ctx", hop_index + 1) for hop_index in range(reach)
    ]
    key_parts = []
    value_parts = []
    for hop_index in range(reach - 1, -1, -1):
        source = chain_pos - (hop_index + 1)
        offset = jnp.maximum(WINDOW + source * row_count, 0)
        cached_keys = lax.dynamic_slice_in_dim(prior_keys, offset, row_count, 0)
        cached_values = lax.dynamic_slice_in_dim(prior_values, offset, row_count, 0)
        key_parts.append(jnp.where(source < 0, cached_keys, earlier[hop_index][0]))
        value_parts.append(jnp.where(source < 0, cached_values, earlier[hop_index][1]))
    key_parts.append(key_rows)
    value_parts.append(value_rows)
    span = (reach + 1) * row_count
    all_keys = jnp.concatenate(key_parts, axis=0).reshape(span, local_kv, HD)
    all_values = jnp.concatenate(value_parts, axis=0).reshape(span, local_kv, HD)
    key_anchor = WINDOW + (chain_pos - reach) * row_count
    query_grouped = query.reshape(row_count, local_kv, group, HD)
    scores = jnp.einsum(
        "qhgd,khd->hgqk", query_grouped, all_keys, preferred_element_type=jnp.float32
    )
    key_pos = key_anchor + jnp.arange(span, dtype=jnp.int32)
    first_valid = WINDOW - stretch_start[0]
    allowed = (
        (key_pos[None, :] <= positions[:, None])
        & (key_pos[None, :] > positions[:, None] - WINDOW)
        & (key_pos[None, :] >= first_valid)
    )
    scores = jnp.where(allowed[None, None, :, :], scores, jnp.float32(-1e30))
    largest = jnp.max(scores, axis=-1, keepdims=True)
    expon = jnp.exp(scores - largest)
    attn_probs = (expon / jnp.sum(expon, axis=-1, keepdims=True)).astype(jnp.bfloat16)
    attended = jnp.einsum(
        "hgqk,khd->qhgd", attn_probs, all_values, preferred_element_type=jnp.float32
    )
    attended = attended.astype(jnp.bfloat16).reshape(row_count, query_cols)
    partial_rows = jnp.dot(
        attended,
        lax.all_gather(o_weight, "ctx", axis=1, tiled=True),
        preferred_element_type=jnp.float32,
    )
    summed = lax.psum_scatter(
        partial_rows.astype(jnp.bfloat16), "tp", scatter_dimension=0, tiled=True
    ).astype(jnp.float32)
    return (residual_in + rms_scale(summed, post_gain)).astype(jnp.bfloat16)


def solution(mesh):
    return jax.shard_map(
        local,
        mesh=mesh,
        in_specs=(
            P(("ctx", "tp"), None),
            P(),
            P(),
            P("ctx", "tp"),
            P("ctx", "tp"),
            P("ctx", "tp"),
            P("tp", "ctx"),
            P(),
            P(),
            P(None, "tp"),
            P(None, "tp"),
            P(),
        ),
        out_specs=P(("ctx", "tp"), None),
        check_vma=False,
    )
```

profile of v0, /device:TPU:0, one launch (start us, length us, event | category | flops | bytes accessed | tf_op | source)
XLA Modules:
  0.0 664.7 jit_solution(9965920459729933018)
XLA Ops:
  6.5 0.0 all-gather.6.cloned.1.call-start
  6.5 1.7 fusion.9
  8.2 2.8 fusion.11
  11.0 0.0 all-gather.6.cloned.1.call-update
  11.1 0.0 all-gather.8.cloned.1.call-start
  11.1 0.7 all-gather.8.cloned.1.call-update
  11.8 0.0 all-gather.10.cloned.1.call-start
  11.9 0.7 all-gather.10.cloned.1.call-update
  12.6 0.0 all-gather.12.cloned.1.call-start
  12.6 0.5 all-gather.12.cloned.1.call-update
  13.1 0.0 all-gather.14.cloned.1.call-start
  13.2 0.5 all-gather.14.cloned.1.call-update
  13.7 0.0 reduce-scatter.2.cloned.1.call-start
  14.5 1.0 multiply_cosine_fusion
  15.5 1.9 and_and_fusion
  17.4 38.5 %all-gather.6.cloned.1.call-done = bf16[512,5376]{1,0:T(8,128)(2,1)} async-done(((bf16[128,5376]{1,0:T(8,128)(2,1)}), bf16[512,5376]{1,0:T(8,128)(2,1)}) %all-gather.6.cloned.1.call-update) | async-done | bytes 5505040 | tf_op jit(solution)/shard_map/all_gather | solution.py:52
  55.8 91.3 %all-gather.8.cloned.1.call-done = bf16[5376,512]{1,0:T(8,128)(2,1)} async-done(((bf16[672,512]{1,0:T(8,128)(2,1)}), bf16[5376,512]{1,0:T(8,128)(2,1)}) %all-gather.8.cloned.1.call-update) | async-done | bytes 5505040 | tf_op jit(solution)/shard_map/all_gather | solution.py:62
  147.2 8.0 %convolution_convert_fusion.1 = bf16[512,512]{1,0:T(8,128)(2,1)} fusion(bf16[512,5376]{1,0:T(8,128)(2,1)} %all-gather.6.cloned.1.call-done, bf16[5376,512]{1,0:T(8,128)(2,1)} %all-gather.8.cloned.1.call-done), kind=kOutput, calls=%fused_computation.32 | convolution fusion | flops 2818834432 | bytes 11534336 | tf_op jit(solution)/shard_map/dot_general | solution.py:58
  155.2 3.4 collective-permute-start
  158.6 3.3 collective-permute-start.1
  161.8 93.2 %all-gather.10.cloned.1.call-done = bf16[5376,512]{1,0:T(8,128)(2,1)} async-done(((bf16[672,512]{1,0:T(8,128)(2,1)}), bf16[5376,512]{1,0:T(8,128)(2,1)}) %all-gather.10.cloned.1.call-update) | async-done | bytes 5505040 | tf_op jit(solution)/shard_map/all_gather | solution.py:61
  255.0 6.7 %multiply_reduce_fusion.1 = (f32[512,4]{0,1:T(4,128)S(1)}, f32[512,512]{0,1:T(8,128)S(1)}) fusion(bf16[512,5376]{1,0:T(8,128)(2,1)} %all-gather.6.cloned.1.call-done, bf16[5376,512]{1,0:T(8,128)(2,1)} %all-gather.10.cloned.1.call-done), kind=kOutput, calls=%fused_computation.37 | convolution fusion | flops 2819094528 | bytes 12066816 | tf_op jit(solution)/shard_map/dot_general | solution.py:58
  261.7 0.3 copy.30
  262.1 0.3 multiply_multiply_fusion.1
  262.4 0.0 copy-start.3
  262.4 0.4 multiply_subtract_fusion.1
  262.9 0.3 copy_bitcast_fusion
  263.2 3.2 collective-permute-start.2
  266.4 3.2 collective-permute-start.3
  269.7 0.3 maximum_convert_fusion
  270.0 0.0 collective-permute-done
  270.0 0.0 collective-permute-done.1
  270.0 0.4 dynamic-slice_select_fusion.1
  270.4 1.1 pad_maximum_fusion
  271.6 1.6 copy.43
  273.2 14.0 %collective-permute-done.2 = bf16[512,512]{1,0:T(8,128)(2,1)} collective-permute-done((bf16[512,512]{1,0:T(8,128)(2,1)S(1)}, bf16[512,512]{1,0:T(8,128)(2,1)}, u32[]{:S(2)}, u32[]{:S(2)}) %collective-permute-start.2) | collective-permute-done | bytes 524320 | tf_op jit(solution)/shard_map/ppermute | solution.py:15
  287.2 3.3 collective-permute-done.3
  290.5 1.6 select_bitcast_fusion.1
  292.1 0.9 copy.51
  293.0 0.9 copy.52
  293.9 138.7 %all-gather.12.cloned.1.call-done = bf16[5376,1024]{1,0:T(8,128)(2,1)} async-done(((bf16[672,1024]{1,0:T(8,128)(2,1)}), bf16[5376,1024]{1,0:T(8,128)(2,1)}) %all-gather.12.cloned.1.call-update) | async-done | bytes 11010064 | tf_op jit(solution)/shard_map/all_gather | solution.py:60
  432.6 10.2 %convolution_bitcast_fusion = f32[64,8,8,128]{3,1,2,0:T(8,128)S(1)} fusion(bf16[512,5376]{1,0:T(8,128)(2,1)} %all-gather.6.cloned.1.call-done, bf16[5376,1024]{1,0:T(8,128)(2,1)} %all-gather.12.cloned.1.call-done), kind=kOutput, calls=%fused_computation.28 | convolution fusion | flops 5637144576 | bytes 18612224 | tf_op jit(solution)/shard_map/dot_general | solution.py:58
  442.8 0.0 copy-start.7
  442.8 0.5 copy.47
  443.3 0.6 multiply_reduce_fusion
  443.9 0.1 copy.34
  444.0 0.1 copy.35
  444.2 0.9 multiply_multiply_fusion
  445.1 1.1 multiply_subtract_fusion
  446.2 0.4 copy.37
  446.6 0.4 copy.36
  447.0 0.0 copy-start.1
  447.0 0.6 fusion.13
  447.6 0.4 copy-done.1
  448.0 0.2 copy-done.2
  448.2 11.9 %fusion.15 = f32[4,1536,512,2]{2,1,3,0:T(8,128)} fusion(bf16[512,4,2,128]{3,0,2,1:T(8,128)(2,1)S(1)} %fusion.13, bf16[512,4,128]{2,0,1:T(8,128)(2,1)S(1)} %maximum_convert_fusion, bf16[512,4,128]{2,0,1:T(8,128)(2,1)S(1)} %bitcast.68, bf16[512,4,128]{2,0,1:T(8,128)(2,1)S(1)} %bitcast.70), kind=kOutput, calls=%fused_computation.38 | convolution fusion | flops 1615331328 | bytes 27787264 | tf_op jit(solution)/shard_map/qhgd,khd->hgqk/dot_general | solution.py:98
  460.1 7.9 %fusion.25 = f32[4,2,512]{2,1,0:T(2,128)S(1)} fusion(pred[512,1536]{0,1:T(8,128)(4,1)S(1)} %copy-done.4, bf16[512,4,2,128]{3,0,2,1:T(8,128)(2,1)S(1)} %fusion.13, bf16[512,4,128]{2,0,1:T(8,128)(2,1)S(1)} %maximum_convert_fusion, bf16[512,4,128]{2,0,1:T(8,128)(2,1)S(1)} %bitcast.69, bf16[512,4,128]{2,0,1:T(8,128)(2,1)S(1)} %bitcast.71), kind=kOutput, calls=%fused_computation.63 | convolution fusion | flops 1634207232 | bytes 3424256 | tf_op jit(solution)/shard_map/sub | solution.py:110
  468.0 13.2 %fusion.14 = bf16[4,128,2,512]{3,1,2,0:T(8,128)(2,1)S(1)} fusion(bf16[1536,4,128,1]{0,2,3,1:T(8,128)(2,1)} %bitcast.72, f32[4,2,512]{2,1,0:T(2,128)S(1)} %fusion.25, f32[4,1536,512,2]{2,1,3,0:T(8,128)} %fusion.15, pred[512,1536]{0,1:T(8,128)(4,1)S(1)} %copy-done.4), kind=kOutput, calls=%fused_computation.31 | convolution fusion | flops 1636308480 | bytes 28590080 | tf_op jit(solution)/shard_map/hgqk,khd->qhgd/dot_general | solution.py:112
  481.2 108.6 %all-gather.14.cloned.1.call-done = bf16[1024,5376]{0,1:T(8,128)(2,1)} async-done(((bf16[1024,672]{0,1:T(8,128)(2,1)}), bf16[1024,5376]{0,1:T(8,128)(2,1)}) %all-gather.14.cloned.1.call-update) | async-done | bytes 11010064 | tf_op jit(solution)/shard_map/all_gather | solution.py:118
  589.8 12.0 %convolution_convert_fusion = bf16[512,5376]{1,0:T(8,128)(2,1)} fusion(bf16[512,1024]{0,1:T(8,128)(2,1)S(1)} %bitcast.74, bf16[1024,5376]{0,1:T(8,128)(2,1)} %all-gather.14.cloned.1.call-done), kind=kOutput, calls=%fused_computation.8 | convolution fusion | flops 5639897088 | bytes 17563648 | tf_op jit(solution)/shard_map/dot_general | solution.py:116
  601.8 0.0 reduce-scatter.2.cloned.1.call-update
  601.8 51.4 %reduce-scatter.2.cloned.1.call-done = bf16[128,5376]{1,0:T(8,128)(2,1)} async-done(((bf16[512,5376]{1,0:T(8,128)(2,1)}), bf16[128,5376]{1,0:T(8,128)(2,1)}) %reduce-scatter.2.cloned.1.call-update) | async-done | bytes 1376272 | tf_op jit(solution)/shard_map/reduce_scatter | solution.py:121
  653.2 1.7 fusion.7
  654.9 3.0 fusion.12
  (20 shorter events, 0.1 us)
Async XLA Ops:
  6.5 49.3 %all-gather.6.cloned.1.call-start = ((), (), s32[]{:S(2)}) async-start(), calls=%async_computation.1 | async-start | bytes 6881280 | tf_op jit(solution)/shard_map/all_gather | solution.py:52
  11.1 136.1 %all-gather.8.cloned.1.call-start = ((), (), s32[]{:S(2)}) async-start(), calls=%async_computation.2 | async-start | bytes 6193152 | tf_op jit(solution)/shard_map/all_gather | solution.py:62
  11.8 243.2 %all-gather.10.cloned.1.call-start = ((), (), s32[]{:S(2)}) async-start(), calls=%async_computation.3 | async-start | bytes 6193152 | tf_op jit(solution)/shard_map/all_gather | solution.py:61
  12.6 420.0 %all-gather.12.cloned.1.call-start = ((), (), s32[]{:S(2)}) async-start(), calls=%async_computation.4 | async-start | bytes 12386304 | tf_op jit(solution)/shard_map/all_gather | solution.py:60
  13.1 576.6 %all-gather.14.cloned.1.call-start = ((), (), s32[]{:S(2)}) async-start(), calls=%async_computation.5 | async-start | bytes 12386304 | tf_op jit(solution)/shard_map/all_gather | solution.py:118
  13.7 639.4 %reduce-scatter.2.cloned.1.call-start = ((), (), s32[]{:S(2)}) async-start(), calls=%async_computation.6 | async-start | bytes 6881280 | tf_op jit(solution)/shard_map/reduce_scatter | solution.py:121
  155.2 106.9 %copy-start.6 = (f32[128]{0:T(128)S(1)}, f32[128]{0:T(128)}, u32[]{:S(2)}) copy-start(f32[128]{0:T(128)} %param.20) | copy-start | bytes 1540
  155.2 114.8 %collective-permute-start = (bf16[512,512]{1,0:T(8,128)(2,1)}, bf16[512,512]{1,0:T(8,128)(2,1)}, u32[]{:S(2)}, u32[]{:S(2)}) collective-permute-start(bf16[512,512]{1,0:T(8,128)(2,1)} %convolution_convert_fusion.1), channel_id=1, source_target_pairs={{0,8},{4,12},{8,16},{12,20},{16,24},{20,28},{1,9},{5,13},{9,17},{1... | collective-permute-start | bytes 1572872 | tf_op jit(solution)/shard_map/ppermute | solution.py:15
  158.6 111.4 %collective-permute-start.1 = (bf16[512,512]{1,0:T(8,128)(2,1)}, bf16[512,512]{1,0:T(8,128)(2,1)}, u32[]{:S(2)}, u32[]{:S(2)}) collective-permute-start(bf16[512,512]{1,0:T(8,128)(2,1)} %convolution_convert_fusion.1), channel_id=1, source_target_pairs={{0,4},{4,8},{8,12},{12,16},{16,20},{20,24},{24,28},{1,5},{5,9},{9,... | collective-permute-start | bytes 1572872 | tf_op jit(solution)/shard_map/ppermute | solution.py:15
  262.4 7.6 %copy-start.3 = (bf16[1024,512]{1,0:T(8,128)(2,1)S(1)}, bf16[1024,512]{1,0:T(8,128)(2,1)}, u32[]{:S(2)}) copy-start(bf16[1024,512]{1,0:T(8,128)(2,1)} %param.22) | copy-start | bytes 3145732
  263.2 24.0 %collective-permute-start.2 = (bf16[512,512]{1,0:T(8,128)(2,1)S(1)}, bf16[512,512]{1,0:T(8,128)(2,1)}, u32[]{:S(2)}, u32[]{:S(2)}) collective-permute-start(bf16[512,512]{1,0:T(8,128)(2,1)S(1)} %copy_bitcast_fusion), channel_id=1, source_target_pairs={{0,8},{4,12},{8,16},{12,20},{16,24},{20,28},{1,9},{5,13},{9,17},{1... | collective-permute-start | bytes 1572872 | tf_op jit(solution)/shard_map/ppermute | solution.py:15
  266.4 24.1 %collective-permute-start.3 = (bf16[512,512]{1,0:T(8,128)(2,1)S(1)}, bf16[512,512]{1,0:T(8,128)(2,1)}, u32[]{:S(2)}, u32[]{:S(2)}) collective-permute-start(bf16[512,512]{1,0:T(8,128)(2,1)S(1)} %copy_bitcast_fusion), channel_id=1, source_target_pairs={{0,4},{4,8},{8,12},{12,16},{16,20},{20,24},{24,28},{1,5},{5,9},{9,... | collective-permute-start | bytes 1572872 | tf_op jit(solution)/shard_map/ppermute | solution.py:15
  442.8 1.4 copy-start.7
  447.0 1.0 copy-start.1
  447.0 1.2 copy-start.2
  448.2 11.9 %copy-start.4 = (pred[512,1536]{0,1:T(8,128)(4,1)S(1)}, pred[512,1536]{0,1:T(8,128)(4,1)}, u32[]{:S(2)}) copy-start(pred[512,1536]{0,1:T(8,128)(4,1)} %and_and_fusion) | copy-start | bytes 2359300
  601.8 53.1 %copy-start = (bf16[128,5376]{1,0:T(8,128)(2,1)S(1)}, bf16[128,5376]{1,0:T(8,128)(2,1)}, u32[]{:S(2)}) copy-start(bf16[128,5376]{1,0:T(8,128)(2,1)} %param.12) | copy-start | bytes 4128772
  601.8 53.1 %copy-start.5 = (f32[5376]{0:T(1024)S(1)}, f32[5376]{0:T(1024)}, u32[]{:S(2)}) copy-start(f32[5376]{0:T(1024)} %param.23) | copy-start | bytes 64516
Sparse Core Ops, SparseCore 0:
  11.2 44.6 all-gather.5
  58.0 89.1 all-gather.7
  149.4 105.6 all-gather.9
  257.0 175.5 all-gather.11
  434.6 155.0 all-gather.13
  601.9 51.2 reduce-scatter.1
where the time goes:
time: 665 us
  waiting for transfers between devices  541 us (81%)
  matrix products  69.9 us (11%)
  other arithmetic  19.8 us (3%)
  between operations  14.4 us (2%)
  starting transfers between devices  13.4 us (2%)
    all_gather x1, waiting for transfers between devices, local(): query_raw = add_piece(lax.all_gather(q_weight, 'ctx', axis=0, tiled=True))  139 us
    all_gather x1, waiting for transfers between devices, local(): lax.all_gather(o_weight, 'ctx', axis=1, tiled=True)  109 us
    all_gather x1, waiting for transfers between devices, local(): key_raw = add_piece(lax.all_gather(k_weight, 'ctx', axis=0, tiled=True))  93.2 us
    all_gather x1, waiting for transfers between devices, local(): value_raw = add_piece(lax.all_gather(v_weight, 'ctx', axis=0, tiled=True))  91.3 us
    reduce_scatter x1, waiting for transfers between devices, local(): lax.psum_scatter(partial_rows.astype(jnp.bfloat16), 'tp', scatter_dimensi...  51.4 us
    all_gather x1, waiting for transfers between devices, local(): block_rows = lax.all_gather(normed, 'tp', axis=0, tiled=True)  38.5 us
    dot_general x3, matrix products, add_piece(): return jnp.dot(block_rows, segment, preferred_element_type=jnp.float32)  24.9 us
    ppermute x4, waiting for transfers between devices, from_behind(): lax.ppermute(value, axis, [(source, source + steps) for source in range(l...  17.3 us
  transfers between devices with their start and end apart: 10, of which 8 were waited for; matrix products, arithmetic and copies ran while one was open for 11% of the time, Pallas kernels for 0%

commit v1 on v0

--- a/solution.py
+++ b/solution.py
@@ -7,6 +7,12 @@
 WINDOW = 1024
 EPSILON = 1e-06
 QUERY_FACTOR = 168.0 ** (-0.5)
+
+
+def gather_blocks(value, mesh_axis, along):
+    shards = lax.all_gather(value, mesh_axis, axis=0, tiled=False)
+    whole = jnp.concatenate(shards, axis=along)
+    return whole
 
 
 def from_behind(value, axis, steps):
@@ -114,9 +120,7 @@
     )
     attended = attended.astype(jnp.bfloat16).reshape(row_count, query_cols)
     partial_rows = jnp.dot(
-        attended,
-        lax.all_gather(o_weight, "ctx", axis=1, tiled=True),
-        preferred_element_type=jnp.float32,
+        attended, gather_blocks(o_weight, "ctx", 1), preferred_element_type=jnp.float32
     )
     summed = lax.psum_scatter(
         partial_rows.astype(jnp.bfloat16), "tp", scatter_dimension=0, tiled=True

time: 665 us -> 697 us (1.048)
  local copies, waits for them, and re-layouts: 5.81 us -> 24.5 us
  waiting for transfers between devices: 541 us -> 555 us
    all_gather x1, waiting for transfers between devices: 109 us -> 122 us  [gather_blocks(): shards = lax.all_gather(value, mesh_axis, axis=0, tiled=False)]
    unnamed x17 -> x20, local copies, waits for them, and re-layouts: 1.07 us -> 11.9 us
    reshape x0 -> x1, local copies, waits for them, and re-layouts: none -> 7.85 us  [gather_blocks(): whole = jnp.concatenate(shards, axis=along)]
  transfers between devices with their start and end apart: 10 -> 10, of which waited for: 8 -> 8; matrix products, arithmetic and copies ran while one was open for 11% -> 9% of each run, Pallas kernels for 0% -> 0%
where the time goes in v1:
time: 697 us; the launch traced here: 696 us
  waiting for transfers between devices  555 us (80%)
  matrix products  69.7 us (10%)
  local copies, waits for them, and re-layouts  24.5 us (4%)
  other arithmetic  19.8 us (3%)
  between operations  14.4 us (2%)
  starting transfers between devices  13.4 us (2%)
    all_gather x1, waiting for transfers between devices, local(): query_raw = add_piece(lax.all_gather(q_weight, 'ctx', axis=0, tiled=True))  139 us
    all_gather x1, waiting for transfers between devices, gather_blocks(): shards = lax.all_gather(value, mesh_axis, axis=0, tiled=False)  122 us
    all_gather x1, waiting for transfers between devices, local(): key_raw = add_piece(lax.all_gather(k_weight, 'ctx', axis=0, tiled=True))  93.2 us
    all_gather x1, waiting for transfers between devices, local(): value_raw = add_piece(lax.all_gather(v_weight, 'ctx', axis=0, tiled=True))  91.3 us
    reduce_scatter x1, waiting for transfers between devices, local(): lax.psum_scatter(partial_rows.astype(jnp.bfloat16), 'tp', scatter_dimensi...  51.4 us
    all_gather x1, waiting for transfers between devices, local(): block_rows = lax.all_gather(normed, 'tp', axis=0, tiled=True)  38.5 us
    dot_general x3, matrix products, add_piece(): return jnp.dot(block_rows, segment, preferred_element_type=jnp.float32)  24.9 us
    ppermute x4, waiting for transfers between devices, from_behind(): lax.ppermute(value, axis, [(source, source + steps) for source in range(l...  17.3 us
  transfers between devices with their start and end apart: 10, of which 8 were waited for; matrix products, arithmetic and copies ran while one was open for 9% of the time, Pallas kernels for 0%

profile of v1, /device:TPU:0, one launch (start us, length us, event | category | flops | bytes accessed | tf_op | source)
XLA Modules:
  0.0 696.4 jit_solution(17433707496782265967)
XLA Ops:
  6.5 1.7 fusion.9
  8.2 2.8 fusion.11
  11.0 0.0 all-gather.7.cloned.1.call-update
  11.1 0.0 all-gather.9.cloned.1.call-start
  11.1 0.7 all-gather.9.cloned.1.call-update
  11.8 0.0 all-gather.11.cloned.1.call-start
  11.9 0.7 all-gather.11.cloned.1.call-update
  12.6 0.0 all-gather.13.cloned.1.call-start
  12.6 0.5 all-gather.13.cloned.1.call-update
  13.1 0.0 all-gather.15.cloned.1.call-start
  13.2 0.5 all-gather.15.cloned.1.call-update
  13.7 0.0 reduce-scatter.2.cloned.1.call-start
  14.5 1.0 multiply_cosine_fusion
  15.5 1.9 and_and_fusion
  17.4 38.5 %all-gather.7.cloned.1.call-done = bf16[512,5376]{1,0:T(8,128)(2,1)} async-done(((bf16[128,5376]{1,0:T(8,128)(2,1)}), bf16[512,5376]{1,0:T(8,128)(2,1)}) %all-gather.7.cloned.1.call-update) | async-done | bytes 5505040 | tf_op jit(solution)/shard_map/all_gather | solution.py:58
  55.8 91.3 %all-gather.9.cloned.1.call-done = bf16[5376,512]{1,0:T(8,128)(2,1)} async-done(((bf16[672,512]{1,0:T(8,128)(2,1)}), bf16[5376,512]{1,0:T(8,128)(2,1)}) %all-gather.9.cloned.1.call-update) | async-done | bytes 5505040 | tf_op jit(solution)/shard_map/all_gather | solution.py:68
  147.2 8.0 %convolution_convert_fusion.1 = bf16[512,512]{1,0:T(8,128)(2,1)} fusion(bf16[512,5376]{1,0:T(8,128)(2,1)} %all-gather.7.cloned.1.call-done, bf16[5376,512]{1,0:T(8,128)(2,1)} %all-gather.9.cloned.1.call-done), kind=kOutput, calls=%fused_computation.32 | convolution fusion | flops 2818834432 | bytes 11534336 | tf_op jit(solution)/shard_map/dot_general | solution.py:64
  155.2 3.4 collective-permute-start
  158.6 3.3 collective-permute-start.1
  161.8 93.2 %all-gather.11.cloned.1.call-done = bf16[5376,512]{1,0:T(8,128)(2,1)} async-done(((bf16[672,512]{1,0:T(8,128)(2,1)}), bf16[5376,512]{1,0:T(8,128)(2,1)}) %all-gather.11.cloned.1.call-update) | async-done | bytes 5505040 | tf_op jit(solution)/shard_map/all_gather | solution.py:67
  255.0 6.7 multiply_reduce_fusion.1
  261.7 0.3 copy.48
  262.1 0.3 multiply_multiply_fusion.1
  262.4 0.0 copy-start.4
  262.4 0.4 multiply_subtract_fusion.1
  262.9 0.3 copy_bitcast_fusion
  263.2 3.3 collective-permute-start.2
  266.4 3.3 collective-permute-start.3
  269.7 0.3 maximum_convert_fusion
  270.0 0.0 collective-permute-done
  270.0 0.4 dynamic-slice_select_fusion.1
  270.4 1.1 pad_maximum_fusion
  271.6 1.6 copy.62
  273.2 14.0 %collective-permute-done.2 = bf16[512,512]{1,0:T(8,128)(2,1)} collective-permute-done((bf16[512,512]{1,0:T(8,128)(2,1)S(1)}, bf16[512,512]{1,0:T(8,128)(2,1)}, u32[]{:S(2)}, u32[]{:S(2)}) %collective-permute-start.2) | collective-permute-done | bytes 524320 | tf_op jit(solution)/shard_map/ppermute | solution.py:21
  287.2 3.3 collective-permute-done.3
  290.5 1.6 select_bitcast_fusion.1
  292.1 0.9 copy.71
  293.0 0.9 copy.72
  293.9 138.7 %all-gather.13.cloned.1.call-done = bf16[5376,1024]{1,0:T(8,128)(2,1)} async-done(((bf16[672,1024]{1,0:T(8,128)(2,1)}), bf16[5376,1024]{1,0:T(8,128)(2,1)}) %all-gather.13.cloned.1.call-update) | async-done | bytes 11010064 | tf_op jit(solution)/shard_map/all_gather | solution.py:66
  432.6 10.2 %convolution_bitcast_fusion = f32[64,8,8,128]{3,1,2,0:T(8,128)S(1)} fusion(bf16[512,5376]{1,0:T(8,128)(2,1)} %all-gather.7.cloned.1.call-done, bf16[5376,1024]{1,0:T(8,128)(2,1)} %all-gather.13.cloned.1.call-done), kind=kOutput, calls=%fused_computation.28 | convolution fusion | flops 5637144576 | bytes 18612224 | tf_op jit(solution)/shard_map/dot_general | solution.py:64
  442.8 0.0 copy-start.8
  442.8 0.5 copy.66
  443.3 0.6 multiply_reduce_fusion
  443.9 0.1 copy.52
  444.0 0.1 copy.53
  444.2 0.9 multiply_multiply_fusion
  445.1 1.1 multiply_subtract_fusion
  446.2 0.4 copy.55
  446.6 0.4 copy.54
  447.0 0.0 copy-start.1
  447.0 0.6 fusion.13
  447.6 0.4 copy-done.1
  448.0 0.2 copy-done.2
  448.2 11.9 %fusion.15 = f32[4,1536,512,2]{2,1,3,0:T(8,128)} fusion(bf16[512,4,2,128]{3,0,2,1:T(8,128)(2,1)S(1)} %fusion.13, bf16[512,4,128]{2,0,1:T(8,128)(2,1)S(1)} %maximum_convert_fusion, bf16[512,4,128]{2,0,1:T(8,128)(2,1)S(1)} %bitcast.78, bf16[512,4,128]{2,0,1:T(8,128)(2,1)S(1)} %bitcast.80), kind=kOutput, calls=%fused_computation.38 | convolution fusion | flops 1615331328 | bytes 27787264 | tf_op jit(solution)/shard_map/qhgd,khd->hgqk/dot_general | solution.py:104
  460.1 7.9 %fusion.25 = f32[4,2,512]{2,1,0:T(2,128)S(1)} fusion(pred[512,1536]{0,1:T(8,128)(4,1)S(1)} %copy-done.5, bf16[512,4,2,128]{3,0,2,1:T(8,128)(2,1)S(1)} %fusion.13, bf16[512,4,128]{2,0,1:T(8,128)(2,1)S(1)} %maximum_convert_fusion, bf16[512,4,128]{2,0,1:T(8,128)(2,1)S(1)} %bitcast.79, bf16[512,4,128]{2,0,1:T(8,128)(2,1)S(1)} %bitcast.81), kind=kOutput, calls=%fused_computation.63 | convolution fusion | flops 1634207232 | bytes 3424256 | tf_op jit(solution)/shard_map/sub | solution.py:116
  468.0 121.8 %all-gather.15.cloned.1.call-done = bf16[8192,672]{0,1:T(8,128)(2,1)} async-done(((bf16[1024,672]{0,1:T(8,128)(2,1)}), bf16[8192,672]{0,1:T(8,128)(2,1)}) %all-gather.15.cloned.1.call-update) | async-done | bytes 11010064 | tf_op jit(solution)/shard_map/all_gather | solution.py:13
  589.8 10.9 %copy.67 = bf16[84,8,8,1024]{3,2,1,0:T(8,128)(2,1)S(1)} copy(bf16[84,8,8,1024]{3,1,2,0:T(8,128)(2,1)} %bitcast.74) | data formatting | bytes 22020096
  600.6 7.9 %copy.58 = bf16[1024,8,672]{0,2,1:T(8,128)(2,1)} copy(bf16[1024,8,672]{0,1,2:T(8,128)(2,1)S(1)} %bitcast.72) | data formatting | bytes 22020096 | tf_op jit(solution)/shard_map/reshape | solution.py:14
  608.5 12.7 %fusion.14 = bf16[4,128,2,512]{3,1,2,0:T(8,128)(2,1)S(1)} fusion(bf16[1536,4,128,1]{0,2,3,1:T(8,128)(2,1)S(1)} %bitcast.82, f32[4,2,512]{2,1,0:T(2,128)S(1)} %fusion.25, f32[4,1536,512,2]{2,1,3,0:T(8,128)} %fusion.15, pred[512,1536]{0,1:T(8,128)(4,1)S(1)} %copy-done.5), kind=kOutput, calls=%fused_computation.31 | convolution fusion | flops 1636308480 | bytes 28590080 | tf_op jit(solution)/shard_map/hgqk,khd->qhgd/dot_general | solution.py:118
  621.2 12.3 %convolution_convert_fusion = bf16[512,5376]{1,0:T(8,128)(2,1)} fusion(bf16[512,1024]{0,1:T(8,128)(2,1)S(1)} %bitcast.84, bf16[1024,5376]{0,1:T(8,128)(2,1)} %bitcast.75), kind=kOutput, calls=%fused_computation.8 | convolution fusion | flops 5639897088 | bytes 17563648 | tf_op jit(solution)/shard_map/dot_general | solution.py:122
  633.4 0.0 reduce-scatter.2.cloned.1.call-update
  633.5 51.4 %reduce-scatter.2.cloned.1.call-done = bf16[128,5376]{1,0:T(8,128)(2,1)} async-done(((bf16[512,5376]{1,0:T(8,128)(2,1)}), bf16[128,5376]{1,0:T(8,128)(2,1)}) %reduce-scatter.2.cloned.1.call-update) | async-done | bytes 1376272 | tf_op jit(solution)/shard_map/reduce_scatter | solution.py:125
  684.8 1.7 fusion.7
  686.6 3.0 fusion.12
  (24 shorter events, 0.1 us)
Async XLA Ops:
  6.5 49.3 %all-gather.7.cloned.1.call-start = ((), (), s32[]{:S(2)}) async-start(), calls=%async_computation.1 | async-start | bytes 6881280 | tf_op jit(solution)/shard_map/all_gather | solution.py:58
  11.1 136.1 %all-gather.9.cloned.1.call-start = ((), (), s32[]{:S(2)}) async-start(), calls=%async_computation.2 | async-start | bytes 6193152 | tf_op jit(solution)/shard_map/all_gather | solution.py:68
  11.8 243.2 %all-gather.11.cloned.1.call-start = ((), (), s32[]{:S(2)}) async-start(), calls=%async_computation.3 | async-start | bytes 6193152 | tf_op jit(solution)/shard_map/all_gather | solution.py:67
  12.6 420.0 %all-gather.13.cloned.1.call-start = ((), (), s32[]{:S(2)}) async-start(), calls=%async_computation.4 | async-start | bytes 12386304 | tf_op jit(solution)/shard_map/all_gather | solution.py:66
  13.1 576.6 %all-gather.15.cloned.1.call-start = ((), (), s32[]{:S(2)}) async-start(), calls=%async_computation.6 | async-start | bytes 12386304 | tf_op jit(solution)/shard_map/all_gather | solution.py:13
  13.7 671.1 %reduce-scatter.2.cloned.1.call-start = ((), (), s32[]{:S(2)}) async-start(), calls=%async_computation.5 | async-start | bytes 6881280 | tf_op jit(solution)/shard_map/reduce_scatter | solution.py:125
  155.2 106.9 %copy-start.7 = (f32[128]{0:T(128)S(1)}, f32[128]{0:T(128)}, u32[]{:S(2)}) copy-start(f32[128]{0:T(128)} %param.20) | copy-start | bytes 1540
  155.2 114.8 %collective-permute-start = (bf16[512,512]{1,0:T(8,128)(2,1)}, bf16[512,512]{1,0:T(8,128)(2,1)}, u32[]{:S(2)}, u32[]{:S(2)}) collective-permute-start(bf16[512,512]{1,0:T(8,128)(2,1)} %convolution_convert_fusion.1), channel_id=1, source_target_pairs={{0,8},{4,12},{8,16},{12,20},{16,24},{20,28},{1,9},{5,13},{9,17},{1... | collective-permute-start | bytes 1572872 | tf_op jit(solution)/shard_map/ppermute | solution.py:21
  158.6 111.4 %collective-permute-start.1 = (bf16[512,512]{1,0:T(8,128)(2,1)}, bf16[512,512]{1,0:T(8,128)(2,1)}, u32[]{:S(2)}, u32[]{:S(2)}) collective-permute-start(bf16[512,512]{1,0:T(8,128)(2,1)} %convolution_convert_fusion.1), channel_id=1, source_target_pairs={{0,4},{4,8},{8,12},{12,16},{16,20},{20,24},{24,28},{1,5},{5,9},{9,... | collective-permute-start | bytes 1572872 | tf_op jit(solution)/shard_map/ppermute | solution.py:21
  262.4 7.6 %copy-start.4 = (bf16[1024,512]{1,0:T(8,128)(2,1)S(1)}, bf16[1024,512]{1,0:T(8,128)(2,1)}, u32[]{:S(2)}) copy-start(bf16[1024,512]{1,0:T(8,128)(2,1)} %param.22) | copy-start | bytes 3145732
  263.2 24.0 %collective-permute-start.2 = (bf16[512,512]{1,0:T(8,128)(2,1)S(1)}, bf16[512,512]{1,0:T(8,128)(2,1)}, u32[]{:S(2)}, u32[]{:S(2)}) collective-permute-start(bf16[512,512]{1,0:T(8,128)(2,1)S(1)} %copy_bitcast_fusion), channel_id=1, source_target_pairs={{0,8},{4,12},{8,16},{12,20},{16,24},{20,28},{1,9},{5,13},{9,17},{1... | collective-permute-start | bytes 1572872 | tf_op jit(solution)/shard_map/ppermute | solution.py:21
  266.4 24.0 %collective-permute-start.3 = (bf16[512,512]{1,0:T(8,128)(2,1)S(1)}, bf16[512,512]{1,0:T(8,128)(2,1)}, u32[]{:S(2)}, u32[]{:S(2)}) collective-permute-start(bf16[512,512]{1,0:T(8,128)(2,1)S(1)} %copy_bitcast_fusion), channel_id=1, source_target_pairs={{0,4},{4,8},{8,12},{12,16},{16,20},{20,24},{24,28},{1,5},{5,9},{9,... | collective-permute-start | bytes 1572872 | tf_op jit(solution)/shard_map/ppermute | solution.py:21
  442.8 1.4 copy-start.8
  447.0 1.0 copy-start.1
  447.0 1.2 copy-start.2
  448.2 11.9 %copy-start.5 = (pred[512,1536]{0,1:T(8,128)(4,1)S(1)}, pred[512,1536]{0,1:T(8,128)(4,1)}, u32[]{:S(2)}) copy-start(pred[512,1536]{0,1:T(8,128)(4,1)} %and_and_fusion) | copy-start | bytes 2359300
  600.6 7.9 %copy-start.3 = (bf16[1536,512]{0,1:T(8,128)(2,1)S(1)}, bf16[1536,512]{0,1:T(8,128)(2,1)}, u32[]{:S(2)}) copy-start(bf16[1536,512]{0,1:T(8,128)(2,1)} %copy.62) | copy-start | bytes 4718596
  633.4 53.1 %copy-start = (bf16[128,5376]{1,0:T(8,128)(2,1)S(1)}, bf16[128,5376]{1,0:T(8,128)(2,1)}, u32[]{:S(2)}) copy-start(bf16[128,5376]{1,0:T(8,128)(2,1)} %param.12) | copy-start | bytes 4128772
  633.4 53.1 %copy-start.6 = (f32[5376]{0:T(1024)S(1)}, f32[5376]{0:T(1024)}, u32[]{:S(2)}) copy-start(f32[5376]{0:T(1024)} %param.23) | copy-start | bytes 64516
Sparse Core Ops, SparseCore 0:
  11.2 44.6 all-gather.6
  58.0 89.1 all-gather.8
  149.4 105.6 all-gather.10
  257.0 175.5 all-gather.12
  434.6 155.0 all-gather.14
  633.6 51.2 reduce-scatter.1
